TPU v7x, 128 devices: a whole 4x4x4 slice. The times are simulated.
128 devices in a mesh: grp: 2 (over core), dev: 64 (over y, x, z).
Axes of the slice: x: 4, y: 4, z: 4, core: 2. Of those that a mesh axis runs over, the one named last changes fastest.
Arguments:
- accum: float32 [16384, 24, 128], P(('grp', 'dev')), may hold values from -48 to 48
- step_count: int32 [24], replicated, may hold values from 1 to 12
- stretch_slot: int32 [16384], replicated, may hold values from 0 to 16383, as said below
- span_length: int32 [128], replicated, may hold values from 1 to 256, 16384 in all
- wet_mask: int32 [32768], P(('grp', 'dev')), may hold values 0 or 1
Outputs:
- ocean_flux: float32 [32768, 24, 128], P(('grp', 'dev'))
Inputs may be any that keep to these rules, and one draw needn't show every extreme that they name: `stretch_slot`: A permutation of the slots; any 128 consecutive row blocks lie on 128 different atmosphere devices (slot // 128). `span_length`: sums to 16384; some ocean device owns exactly 256 blocks. `wet_mask`: entries of slots beyond an ocean device's span are ignored.
All inputs are finite; a program needn't handle non-finite values.
Results may differ from a plain program's by a relative error of at most 0.000071.
Values sent between devices are 32-bit elements; how exact they have to be, the bound alone decides.
A program may use at most 64 MiB of HBM per device.

v0:
```python
import jax
import jax.numpy as jnp
from jax import lax
from jax.sharding import PartitionSpec as P


def passed_along(value, axis, steps):
    count = lax.axis_size(axis)
    initial, last = (max(0, -steps), min(count, count - steps))
    return lax.ppermute(value, axis, [(source, source + steps) for source in range(initial, last)])


def select_rows(picks, table):
    return jnp.dot(
        picks, table, precision=lax.Precision.HIGHEST, preferred_element_type=jnp.float32
    )


def on_device(accum, step_count, stretch_slot, span_length, wet_mask):
    devices = lax.axis_size(("grp", "dev"))
    my_index = lax.axis_index(("grp", "dev"))
    blocks_dev = accum.shape[0]
    fields = accum.shape[1]
    cells = accum.shape[2]
    capacity = wet_mask.shape[0]
    pair_most = capacity // devices
    all_blocks = stretch_slot.shape[0]
    span_end = jnp.cumsum(span_length)
    span_start = span_end - span_length
    all_ids = jnp.arange(all_blocks, dtype=jnp.int32)
    local_ids = jnp.arange(blocks_dev, dtype=jnp.int32)
    mine = stretch_slot[None, :] == (my_index * blocks_dev + local_ids)[:, None]
    my_global = jnp.sum(jnp.where(mine, all_ids[None, :], 0), axis=1)
    owner = jnp.sum((span_end[None, :] <= my_global[:, None]).astype(jnp.int32), axis=1)
    same_owner = owner[:, None] == owner[None, :]
    earlier = my_global[None, :] < my_global[:, None]
    order_in = jnp.sum((same_owner & earlier).astype(jnp.int32), axis=1)
    position = owner * pair_most + order_in
    buffer_ids = jnp.arange(devices * pair_most, dtype=jnp.int32)
    send_picks = (position[None, :] == buffer_ids[:, None]).astype(jnp.float32)
    counts = step_count.astype(jnp.float32)
    normal = (accum / counts[None, :, None]).reshape(blocks_dev, fields * cells)
    sendbuf = select_rows(send_picks, normal).reshape(devices, pair_most, fields, cells)
    received = lax.all_to_all(sendbuf, ("grp", "dev"), split_axis=0, concat_axis=0, tiled=True)
    received = received.reshape(devices * pair_most, fields * cells)
    length = span_length[my_index]
    start = span_start[my_index]
    slots = jnp.arange(capacity, dtype=jnp.int32)
    valid = slots < length
    global_ids = jnp.minimum(start + slots, all_blocks - 1)
    sender = stretch_slot[global_ids] // blocks_dev
    same_sender = (sender[:, None] == sender[None, :]) & valid[None, :]
    lower = slots[None, :] < slots[:, None]
    rank_in = jnp.sum((same_sender & lower).astype(jnp.int32), axis=1)
    place_ids = sender * pair_most + rank_in
    place_picks = (place_ids[:, None] == buffer_ids[None, :]).astype(jnp.float32)
    placed = select_rows(place_picks, received).reshape(capacity, fields, cells)
    wet = (valid & (wet_mask == 1)).astype(jnp.float32)
    masked = placed * wet[:, None, None]
    last_cells = masked[:, :, cells - 1]
    first_cells = masked[:, :, 0]
    last_cell = lax.dynamic_index_in_dim(last_cells, length - 1, 0, keepdims=False)
    first_cell = first_cells[0]
    left_in = passed_along(last_cell, ("grp", "dev"), 1)
    right_in = passed_along(first_cell, ("grp", "dev"), -1)
    before_col = jnp.concatenate([left_in[None, :], last_cells[:-1]], axis=0)
    after_col = jnp.concatenate([first_cells[1:], jnp.zeros((1, fields), jnp.float32)], axis=0)
    after_col = jnp.where((slots == length - 1)[:, None], right_in[None, :], after_col)
    cell_ids = jnp.arange(cells, dtype=jnp.int32)
    distance = jnp.abs(cell_ids[:, None] - cell_ids[None, :])
    stencil = jnp.where(distance == 0, 0.5, jnp.where(distance == 1, 0.25, 0.0)).astype(jnp.float32)
    inner = jnp.dot(
        masked.reshape(capacity * fields, cells),
        stencil,
        precision=lax.Precision.HIGHEST,
        preferred_element_type=jnp.float32,
    ).reshape(capacity, fields, cells)
    first_hot = (cell_ids == 0).astype(jnp.float32)
    last_hot = (cell_ids == cells - 1).astype(jnp.float32)
    edges_added = (
        0.25 * before_col[:, :, None] * first_hot[None, None, :]
        + 0.25 * after_col[:, :, None] * last_hot[None, None, :]
    )
    smoothed = (inner + edges_added) * wet[:, None, None]
    return smoothed


def solution(mesh):
    return jax.shard_map(
        on_device,
        mesh=mesh,
        in_specs=(P(("grp", "dev"), None, None), P(), P(), P(), P(("grp", "dev"))),
        out_specs=P(("grp", "dev"), None, None),
        check_vma=False,
    )
```

profile of v0, /device:TPU:1, one launch (start us, length us, event | category | flops | bytes accessed | tf_op | source)
XLA Modules:
  0.0 98.8 jit_solution(108615013765676878)
XLA Ops:
  0.0 0.7 convert_element_type.34
  0.7 0.8 copy.31
  1.7 2.2 %select_reduce_fusion = s32[128]{0:T(128)S(1)} fusion(s32[16384]{0:T(1024)} %param.7, s32[128]{0:T(128)S(1)} %iota_add_fusion), kind=kLoop, calls=%fused_computation.1 | loop fusion | flops 6291328 | bytes 66560 | tf_op jit(solution)/shard_map/reduce_sum | solution.py:33
  4.3 1.6 %broadcast_divide_fusion = f32[128,24,128]{2,1,0:T(8,128)S(1)} fusion(f32[128,24,128]{2,1,0:T(8,128)} %param.5, f32[24]{0:T(128)S(1)} %convert_element_type.34), kind=kLoop, calls=%fused_computation.6 | loop fusion | flops 393216 | bytes 3145824 | tf_op jit(solution)/shard_map/div | solution.py:42
  5.8 0.3 copy.52
  6.1 0.5 copy.32
  6.6 1.5 %fusion.4 = f32[128,2,24,128]{3,0,2,1:T(8,128)S(1)} fusion(f32[24,128,128,1]{2,1,0,3:T(8,128)S(1)} %bitcast.50, s32[128,2]{0,1:T(2,128)S(1)} %multiply_add_fusion, s32[128]{0:T(128)S(1)} %multiply_add_fusion.2), kind=kOutput, calls=%fused_computation.13 | convolution fusion | flops 1207992320 | bytes 4720128 | tf_op jit(solution)/shard_map/dot_general | solution.py:14
  8.1 3.5 %copy.33 = f32[128,2,24,128]{3,2,1,0:T(8,128)} copy(f32[128,2,24,128]{3,0,2,1:T(8,128)S(1)} %fusion.4) | data formatting | bytes 6291456 | tf_op jit(solution)/shard_map/dot_general | solution.py:14
  11.6 11.5 %all-to-all-start = ((f32[128,2,24,128]{3,2,1,0:T(8,128)}), f32[128,2,24,128]{3,2,1,0:T(8,128)S(1)}, u32[]{:S(2)}, u32[]{:S(2)}) async-start(f32[128,2,24,128]{3,2,1,0:T(8,128)} %copy.33), calls=%async_computation | async-start | bytes 6291456 | tf_op jit(solution)/shard_map/all_to_all | solution.py:44
  23.1 0.7 dynamic_slice.11
  25.1 0.6 dynamic_slice.10
  25.7 0.6 compare_select_fusion
  26.3 1.7 %gather_fusion = s32[256]{0:T(256)S(1)} fusion(s32[16384]{0:T(1024)S(1)} %copy-done, s32[1024]{0:T(1024)S(1)} %pad_clamp_fusion), kind=kCustom, calls=%fused_computation | custom fusion | bytes 3072 | tf_op jit(solution)/shard_map/gather | solution.py:51
  28.1 0.7 and_convert_fusion
  29.0 33.8 %all-to-all-done = f32[128,2,24,128]{3,2,1,0:T(8,128)S(1)} async-done(((f32[128,2,24,128]{3,2,1,0:T(8,128)}), f32[128,2,24,128]{3,2,1,0:T(8,128)S(1)}, u32[]{:S(2)}, u32[]{:S(2)}) %all-to-all-start) | async-done | bytes 3145760 | tf_op jit(solution)/shard_map/all_to_all | solution.py:44
  62.9 2.2 %copy.51 = f32[32,8,24,128]{3,1,2,0:T(8,128)} copy(f32[32,8,24,128]{3,2,1,0:T(8,128)S(1)} %bitcast.46) | data formatting | bytes 6291456
  65.1 3.5 %copy.34 = f32[3072,256]{1,0:T(8,128)} copy(f32[3072,256]{0,1:T(8,128)} %bitcast.48) | data formatting | bytes 6291456 | tf_op jit(solution)/shard_map/dot_general | solution.py:14
  68.6 3.5 %convolution_multiply_fusion = f32[256,24,128]{0,2,1:T(8,128)S(1)} fusion(f32[24,128,256]{2,1,0:T(8,128)} %bitcast.47, f32[256]{0:T(256)S(1)} %get-tuple-element.7, s32[256]{0:T(256)S(1)} %multiply_add_fusion.1), kind=kOutput, calls=%fused_computation.4 | convolution fusion | flops 2416771072 | bytes 6293504 | tf_op jit(solution)/shard_map/dot_general | solution.py:14
  72.6 6.7 %collective-permute-start.1 = (f32[24]{0:T(128)S(1)}, f32[24]{0:T(128)S(1)}, u32[]{:S(2)}, u32[]{:S(2)}) collective-permute-start(f32[24]{0:T(128)S(1)} %slice_reduce_fusion), channel_id=1, source_target_pairs={{1,0},{2,1},{3,2},{4,3},{5,4},{6,5},{7,6},{8,7},{9,8},{10,9},{11,1... | collective-permute-start | bytes 296 | tf_op jit(solution)/shard_map/ppermute | solution.py:10
  79.2 0.4 dynamic-slice_reduce_fusion
  79.6 2.1 %collective-permute-start = (f32[24]{0:T(128)S(1)}, f32[24]{0:T(128)S(1)}, u32[]{:S(2)}, u32[]{:S(2)}) collective-permute-start(f32[24]{0:T(128)S(1)} %dynamic-slice_reduce_fusion), channel_id=1, source_target_pairs={{0,1},{1,2},{2,3},{3,4},{4,5},{5,6},{6,7},{7,8},{8,9},{9,10},{10,1... | collective-permute-start | bytes 296 | tf_op jit(solution)/shard_map/ppermute | solution.py:10
  81.8 8.2 %collective-permute-done = f32[24]{0:T(128)S(1)} collective-permute-done((f32[24]{0:T(128)S(1)}, f32[24]{0:T(128)S(1)}, u32[]{:S(2)}, u32[]{:S(2)}) %collective-permute-start) | collective-permute-done | bytes 128 | tf_op jit(solution)/shard_map/ppermute | solution.py:10
  90.2 5.1 %add_multiply_fusion = f32[256,24,128]{0,2,1:T(8,128)} fusion(f32[128]{0:T(128)S(1)} %get-tuple-element.9, f32[256,24]{0,1:T(8,128)S(1)} %select_multiply_fusion, f32[128]{0:T(128)S(1)} %get-tuple-element.10, f32[256,24]{0,1:T(8,128)S(1)} %maximum_multiply_fusion, f32[256]{0:T(256)S(1)} %get-tuple-element.7, f32[256,24,128]{0,2,1:T(8,128)S(1)} %convolution_multiply_fusion), kind=kOutput, calls=%fused_computation.3 | convolution fusion | flops 1211990016 | bytes 6342656 | tf_op jit(solution)/shard_map/dot_general | solution.py:72
  95.3 3.5 %copy.39 = f32[256,24,128]{2,1,0:T(8,128)} copy(f32[256,24,128]{0,2,1:T(8,128)} %add_multiply_fusion) | data formatting | bytes 6291456 | tf_op jit(solution)/shard_map/mul | solution.py:84
  (29 shorter events, 1.5 us)
Async XLA Ops:
  11.6 11.5 %copy-start.2 = (s32[128]{0:T(128)S(1)}, s32[128]{0:T(128)}, u32[]{:S(2)}) copy-start(s32[128]{0:T(128)} %param.8) | copy-start | bytes 1540
  11.6 14.7 %copy-start = (s32[16384]{0:T(1024)S(1)}, s32[16384]{0:T(1024)}, u32[]{:S(2)}) copy-start(s32[16384]{0:T(1024)} %param.7) | copy-start | bytes 196612
  11.6 16.5 %copy-start.1 = (s32[256]{0:T(256)S(1)}, s32[256]{0:T(256)}, u32[]{:S(2)}) copy-start(s32[256]{0:T(256)} %param.9) | copy-start | bytes 3076
  11.6 51.3 %all-to-all-start = ((f32[128,2,24,128]{3,2,1,0:T(8,128)}), f32[128,2,24,128]{3,2,1,0:T(8,128)S(1)}, u32[]{:S(2)}, u32[]{:S(2)}) async-start(f32[128,2,24,128]{3,2,1,0:T(8,128)} %copy.33), calls=%async_computation | async-start | bytes 6291456 | tf_op jit(solution)/shard_map/all_to_all | solution.py:44
  72.6 17.5 %collective-permute-start.1 = (f32[24]{0:T(128)S(1)}, f32[24]{0:T(128)S(1)}, u32[]{:S(2)}, u32[]{:S(2)}) collective-permute-start(f32[24]{0:T(128)S(1)} %slice_reduce_fusion), channel_id=1, source_target_pairs={{1,0},{2,1},{3,2},{4,3},{5,4},{6,5},{7,6},{8,7},{9,8},{10,9},{11,1... | collective-permute-start | bytes 296 | tf_op jit(solution)/shard_map/ppermute | solution.py:10
  79.6 10.3 %collective-permute-start = (f32[24]{0:T(128)S(1)}, f32[24]{0:T(128)S(1)}, u32[]{:S(2)}, u32[]{:S(2)}) collective-permute-start(f32[24]{0:T(128)S(1)} %dynamic-slice_reduce_fusion), channel_id=1, source_target_pairs={{0,1},{1,2},{2,3},{3,4},{4,5},{5,6},{6,7},{7,8},{8,9},{9,10},{10,1... | collective-permute-start | bytes 296 | tf_op jit(solution)/shard_map/ppermute | solution.py:10
where the time goes:
time: 99.2 us; the launch traced here: 98.8 us
  waiting for transfers between devices  42 us (42%)
  starting transfers between devices  20.2 us (20%)
  local copies, waits for them, and re-layouts  18.2 us (18%)
  matrix products  10.1 us (10%)
  other arithmetic  6.7 us (7%)
  between operations  1.59 us (2%)
    all_to_all x1, waiting for transfers between devices, on_device(): lax.all_to_all(sendbuf, ('grp', 'dev'), split_axis=0, concat_axis=0, tile...  33.8 us
    all_to_all x1, starting transfers between devices, on_device(): lax.all_to_all(sendbuf, ('grp', 'dev'), split_axis=0, concat_axis=0, tile...  11.5 us
    ppermute x2, starting transfers between devices, passed_along(): lax.ppermute(value, axis, [(source, source + steps) for source in range(i...  8.75 us
    ppermute x2, waiting for transfers between devices, passed_along(): lax.ppermute(value, axis, [(source, source + steps) for source in range(i...  8.19 us
    dot_general x3, local copies, waits for them, and re-layouts, select_rows(): jnp.dot(picks, table, precision=lax.Precision.HIGHEST, preferred_element_...  7.49 us
    dot_general x1, matrix products, on_device(): jnp.dot(masked.reshape(capacity * fields, cells), stencil, precision=lax....  5.09 us
    dot_general x2, matrix products, select_rows(): jnp.dot(picks, table, precision=lax.Precision.HIGHEST, preferred_element_...  5.01 us
    mul x1, local copies, waits for them, and re-layouts, on_device(): smoothed = (inner + edges_added) * wet[:, None, None]  3.54 us
  transfers between devices with their start and end apart: 3, of which 2 were waited for; matrix products, arithmetic and copies ran while one was open for 5% of the time, Pallas kernels for 0%

commit v1 on v0

v1 whole, which is shorter than its diff:
```python
import itertools

import jax
import jax.numpy as jnp
from jax import lax
from jax.experimental import pallas as pl
from jax.experimental.pallas import tpu as pltpu
from jax.sharding import PartitionSpec as P

MESH = pl.DeviceIdType.MESH
SIDE = 4
CHIPS = SIDE**3
DEVICES = 2 * CHIPS
GROUP = 8


DISTANCES = sorted(itertools.product(range(SIDE // 2 + 1), repeat=3), key=lambda d: -sum(d))


def partners_at(distance, me, visit):
    both_ways = [axis for axis, step in enumerate(distance) if step == 1]

    def one(number, carry):
        signs = dict.fromkeys(range(3), 1)
        for bit, axis in enumerate(both_ways):
            signs[axis] = 1 - 2 * ((number // 2 ** (bit + 1)) % 2)
        steps = [distance[axis] * signs[axis] + SIDE for axis in range(3)]
        visit(partner((number % 2, *steps), me))
        return carry

    lax.fori_loop(0 if any(distance) else 1, 2 ** (len(both_ways) + 1), one, 0)


def partner(offset, me):
    core, y, x, z = ((at + step) % size for at, step, size in zip(me, offset, (2, SIDE, SIDE, SIDE)))
    return core, (y * SIDE + x) * SIDE + z


def kernel(
    accum_hbm,
    slot_ref,
    slot_hbm,
    length_ref,
    wet_ref,
    count_ref,
    out_ref,
    accum,
    send,
    recv_0,
    recv_1,
    recv_2,
    edge_send,
    edge_recv,
    picks,
    picks_smem,
    slot_smem,
    from_smem,
    wet_smem,
    last_smem,
    accum_sem,
    picks_sem,
    slot_sem,
    send_sem,
    recv_sem,
    edge_send_sem,
    edge_recv_sem,
):
    groups = send.shape[0]
    recvs = (recv_0, recv_1, recv_2)
    blocks = accum.shape[0]
    core, chip = lax.axis_index("grp"), lax.axis_index("dev")
    me = (core, chip // (SIDE * SIDE), (chip // SIDE) % SIDE, chip % SIDE)
    mine = core * CHIPS + chip

    barrier = pltpu.get_barrier_semaphore()

    def greet(step, carry):
        other = (mine + step) % DEVICES
        pl.semaphore_signal(barrier, 1, device_id=(other // CHIPS, other % CHIPS), device_id_type=MESH)
        return carry

    lax.fori_loop(1, DEVICES, greet, 0)
    accum_copy = pltpu.make_async_copy(accum_hbm, accum, accum_sem)
    accum_copy.start()
    slot_copy = pltpu.make_async_copy(slot_hbm, slot_smem, slot_sem)
    slot_copy.start()

    row = lax.broadcasted_iota(jnp.int32, (128, 128), 0)
    lane = lax.broadcasted_iota(jnp.int32, (128, 128), 1)
    length = length_ref[...]
    length_col = jnp.sum(jnp.where(row == lane, length, 0), axis=1, keepdims=True)
    end = jnp.sum(jnp.where(row <= lane, length_col, 0), axis=0, keepdims=True)
    start = end - length
    slot = slot_ref[...]
    held = (slot >> 7) == mine
    column = jnp.sum(jnp.where(held, lane, 0), axis=1, keepdims=True)
    local = jnp.sum(jnp.where(held, slot & 127, 0), axis=1, keepdims=True)
    order = row * 128 + column - start
    inside = (order >= 0) & (order < length)
    for rank in range(2):
        chosen = inside & ((order >= 128) == (rank == 1))
        picks[rank : rank + 1, :] = jnp.sum(jnp.where(chosen, local, 0), axis=0, keepdims=True)
    picks_copy = pltpu.make_async_copy(picks, picks_smem, picks_sem)
    picks_copy.start()
    at_me = lax.broadcasted_iota(jnp.int32, (1, 128), 1) == mine
    my_start = jnp.sum(jnp.where(at_me, start, 0))
    my_length = jnp.sum(jnp.where(at_me, length, 0))
    picks_copy.wait()
    accum_copy.wait()

    def pack(owner, carry):
        for rank in range(2):
            block = accum[picks_smem[rank, owner]]
            for group in range(groups):
                send[group, owner, rank] = block[group * GROUP : (group + 1) * GROUP]
        return carry

    lax.fori_loop(0, DEVICES, pack, 0, unroll=4)
    for group in range(groups):
        recvs[group][mine] = send[group, mine]
    pl.semaphore_wait(barrier, DEVICES - 1)

    for group in range(groups):

        def post(other, group=group):
            pltpu.make_async_remote_copy(
                src_ref=send.at[group, other[0] * CHIPS + other[1]],
                dst_ref=recvs[group].at[mine],
                send_sem=send_sem,
                recv_sem=recv_sem.at[group],
                device_id=other,
                device_id_type=MESH,
            ).start()

        for distance in DISTANCES:
            partners_at(distance, me, post)

    slot_copy.wait()

    def table(index, carry):
        block = jnp.minimum(my_start + index, DEVICES * blocks - 1)
        from_smem[index] = slot_smem[block >> 7, block & 127] >> 7
        valid = (index < my_length) & (wet_ref[index >> 7, index & 127] == 1)
        wet_smem[index] = jnp.where(valid, 1.0, 0.0)
        last_smem[index] = jnp.where(index == my_length - 1, 1.0, 0.0)
        return carry

    lax.fori_loop(0, 2 * 128, table, 0, unroll=4)

    field_row = lax.broadcasted_iota(jnp.int32, (groups * GROUP, 128), 0)
    field_lane = lax.broadcasted_iota(jnp.int32, (groups * GROUP, 128), 1)
    scale = 1.0 / jnp.sum(
        jnp.where(field_row == field_lane, count_ref[...].astype(jnp.float32), 0.0), axis=1, keepdims=True
    )
    at_lane = lax.broadcasted_iota(jnp.int32, (GROUP, 128), 1)
    first_lane, last_lane = at_lane == 0, at_lane == 127
    has_left = jnp.where(mine > 0, 1.0, 0.0)
    has_right = jnp.where(mine < DEVICES - 1, 1.0, 0.0)
    after, before = (mine + 1) % DEVICES, (mine + DEVICES - 1) % DEVICES
    final = jnp.maximum(my_length, 1) - 1

    for group in range(groups):
        recv = recvs[group]
        arrived = recv.at[pl.ds(0, DEVICES - 1)]
        pltpu.make_async_copy(arrived, arrived, recv_sem.at[group]).wait()
        by_field = jnp.broadcast_to(scale[group * GROUP : (group + 1) * GROUP], (GROUP, 128))
        edge_send[group, 0] = recv[from_smem[final], final >> 7] * by_field * wet_smem[final]
        edge_send[group, 1] = recv[from_smem[0], 0] * by_field * wet_smem[0]
        copies = []
        for side, other in enumerate((after, before)):
            copy = pltpu.make_async_remote_copy(
                src_ref=edge_send.at[group, side],
                dst_ref=edge_recv.at[group, side],
                send_sem=edge_send_sem.at[group, side],
                recv_sem=edge_recv_sem.at[group, side],
                device_id=(other // CHIPS, other % CHIPS),
                device_id_type=MESH,
            )
            copy.start()
            copies.append(copy)
        for copy in copies:
            copy.wait()
        left = pltpu.roll(edge_recv[group, 0], 1, 1) * has_left
        right = pltpu.roll(edge_recv[group, 1], 127, 1) * has_right

        def value(index, rank, recv=recv, by_field=by_field):
            return recv[from_smem[index], rank] * (by_field * wet_smem[index])

        def smooth(index, next_rank, carry):
            current, to_right, to_left, previous = carry
            if next_rank is None:
                following = jnp.zeros_like(current)
            else:
                following = value(index + 1, next_rank)
            next_right, next_left = pltpu.roll(following, 1, 1), pltpu.roll(following, 127, 1)
            before_cell = jnp.where(first_lane, previous, to_right)
            after_cell = jnp.where(last_lane, next_left + last_smem[index] * right, to_left)
            smoothed = 0.5 * current + 0.25 * (before_cell + after_cell)
            out_ref[index, group * GROUP : (group + 1) * GROUP, :] = smoothed * wet_smem[index]
            return following, next_right, next_left, to_right

        current = value(0, 0)
        carry = (current, pltpu.roll(current, 1, 1), pltpu.roll(current, 127, 1), left)
        carry = lax.fori_loop(0, 127, lambda i, c: smooth(i, 0, c), carry)
        carry = lax.fori_loop(127, 255, lambda i, c: smooth(i, 1, c), carry)
        smooth(255, None, carry)

    sent = send.at[0, pl.ds(0, DEVICES - 1)]

    def drain(group, carry):
        pltpu.make_async_copy(sent, sent, send_sem).wait()
        return carry

    lax.fori_loop(0, groups, drain, 0)


def on_device(accum, step_count, stretch_slot, span_length, wet_mask):
    blocks, fields, cells = accum.shape
    capacity = wet_mask.shape[0]
    groups = fields // GROUP
    slots = stretch_slot.reshape(-1, 128)
    counts = jnp.pad(step_count, (0, 128 - fields), constant_values=1).reshape(1, 128)
    vmem, smem, anywhere = (pl.BlockSpec(memory_space=m) for m in (pltpu.VMEM, pltpu.SMEM, pl.ANY))
    return pl.pallas_call(
        kernel,
        out_shape=jax.ShapeDtypeStruct((capacity, fields, cells), jnp.float32),
        in_specs=[anywhere, vmem, anywhere, vmem, smem, vmem],
        out_specs=vmem,
        scratch_shapes=[
            pltpu.VMEM((blocks, fields, cells), jnp.float32),
            pltpu.VMEM((groups, DEVICES, 2, GROUP, cells), jnp.float32),
            *[pltpu.VMEM((DEVICES, 2, GROUP, cells), jnp.float32)] * groups,
            pltpu.VMEM((groups, 2, GROUP, cells), jnp.float32),
            pltpu.VMEM((groups, 2, GROUP, cells), jnp.float32),
            pltpu.VMEM((2, 128), jnp.int32),
            pltpu.SMEM((2, 128), jnp.int32),
            pltpu.SMEM((128, 128), jnp.int32),
            pltpu.SMEM((capacity,), jnp.int32),
            pltpu.SMEM((capacity,), jnp.float32),
            pltpu.SMEM((capacity,), jnp.float32),
            pltpu.SemaphoreType.DMA,
            pltpu.SemaphoreType.DMA,
            pltpu.SemaphoreType.DMA,
            pltpu.SemaphoreType.DMA,
            pltpu.SemaphoreType.DMA((groups,)),
            pltpu.SemaphoreType.DMA((groups, 2)),
            pltpu.SemaphoreType.DMA((groups, 2)),
        ],
        compiler_params=pltpu.CompilerParams(
            collective_id=0, has_side_effects=True, vmem_limit_bytes=32 * 1024 * 1024
        ),
        name="remap",
    )(accum, slots, slots, span_length.reshape(1, -1), wet_mask.reshape(2, -1), counts)


def solution(mesh):
    return jax.shard_map(
        on_device,
        mesh=mesh,
        in_specs=(P(("grp", "dev"), None, None), P(), P(), P(), P(("grp", "dev"))),
        out_specs=P(("grp", "dev"), None, None),
        check_vma=False,
    )
```

time: 99.2 us -> 127 us (1.28)
  Pallas kernels: 0 us -> 120 us
  waiting for transfers between devices: 42 us -> 0 us
  starting transfers between devices: 20.2 us -> 0 us
  local copies, waits for them, and re-layouts: 18.2 us -> 5.9 us
  matrix products: 10.1 us -> 0 us
  other arithmetic: 6.7 us -> 0 us
  between operations: 1.59 us -> 0.01 us
    pallas_call x0 -> x1, Pallas kernels: none -> 120 us  [on_device(): pl.pallas_call(kernel, out_shape=jax.ShapeDtypeStruct((capacity, fields,...]
    all_to_all x1 -> x0, waiting for transfers between devices: 33.8 us -> none  [on_device(): lax.all_to_all(sendbuf, ('grp', 'dev'), split_axis=0, concat_axis=0, tile...]
    all_to_all x1 -> x0, starting transfers between devices: 11.5 us -> none  [on_device(): lax.all_to_all(sendbuf, ('grp', 'dev'), split_axis=0, concat_axis=0, tile...]
    dot_general x3 -> x0, matrix products: 10.1 us -> none  [the longest x1 5.09 us: on_device(): jnp.dot(masked.reshape(capacity * fields, cells), stencil, precision=lax....]
    ppermute x2 -> x0, starting transfers between devices: 8.75 us -> none  [passed_along(): lax.ppermute(value, axis, [(source, source + steps) for source in range(i...]
    ppermute x2 -> x0, waiting for transfers between devices: 8.19 us -> none  [passed_along(): lax.ppermute(value, axis, [(source, source + steps) for source in range(i...]
    dot_general x3 -> x0, local copies, waits for them, and re-layouts: 7.49 us -> none  [select_rows(): jnp.dot(picks, table, precision=lax.Precision.HIGHEST, preferred_element_...]
    mul x1 -> x0, local copies, waits for them, and re-layouts: 3.54 us -> none  [on_device(): smoothed = (inner + edges_added) * wet[:, None, None]]
  transfers between devices with their start and end apart: 3 -> 0, of which waited for: 2 -> 0; matrix products, arithmetic and copies ran while one was open for 5% -> 0% of each run, Pallas kernels for 0% -> 0%
where the time goes in v1:
time: 127 us; the launch traced here: 126 us
  Pallas kernels  120 us (94%)
  local copies, waits for them, and re-layouts  5.9 us (5%)
    pallas_call x1, Pallas kernels, on_device(): pl.pallas_call(kernel, out_shape=jax.ShapeDtypeStruct((capacity, fields,...  120 us
    unnamed x9, local copies, waits for them, and re-layouts  5.25 us

profile of v1, /device:TPU:1, one launch (start us, length us, event | category | flops | bytes accessed | tf_op | source)
XLA Modules:
  0.0 125.7 jit_solution(5416506494233258723)
XLA Ops:
  0.0 0.7 pad_bitcast_fusion.count_ref
  0.7 0.0 copy-start
  0.7 1.4 %copy-done = f32[128,24,128]{2,1,0:T(8,128)S(1)} copy-done((f32[128,24,128]{2,1,0:T(8,128)S(1)}, f32[128,24,128]{2,1,0:T(8,128)}, u32[]{:S(2)}) %copy-start) | copy-done | bytes 1572888
  2.1 0.0 copy-start.1
  2.1 0.8 copy-done.1
  2.9 0.0 copy-start.2
  2.9 0.7 copy-done.2
  3.6 0.0 copy-start.3
  3.6 0.7 copy-done.3
  4.2 119.8 %remap.1 = f32[256,24,128]{2,1,0:T(8,128)S(1)} custom-call(f32[128,24,128]{2,1,0:T(8,128)S(1)} %copy-done, s32[128,128]{1,0:T(8,128)S(1)} %bitcast.5, s32[128,128]{1,0:T(8,128)S(1)} %bitcast.6, s32[1,128]{1,0:T(1,128)S(1)} %bitcast.8, s32[2,128]{1,0:T(2,128)S(1)} %bitcast.7, s32[1,128]{1,0:T(1,128)S(1)} %pad_bitcast_fusion.count_ref), custom_call_target="tpu_custom_call" | custom-call | tf_op jit(solution)/shard_map/remap/pallas_call | solution.py:224
  124.0 1.7 %copy.7 = f32[256,24,128]{2,1,0:T(8,128)} copy(f32[256,24,128]{2,1,0:T(8,128)S(1)} %remap.1) | data formatting | bytes 6291456
Async XLA Ops:
  0.7 1.4 %copy-start = (f32[128,24,128]{2,1,0:T(8,128)S(1)}, f32[128,24,128]{2,1,0:T(8,128)}, u32[]{:S(2)}) copy-start(f32[128,24,128]{2,1,0:T(8,128)} %accum_hbm.1) | copy-start | bytes 4718596
  2.1 0.8 copy-start.1
  2.9 0.7 copy-start.2
  3.6 0.7 copy-start.3

commit v2 on v1

v2 whole, which is shorter than its diff:
```python
import itertools

import jax
import jax.numpy as jnp
from jax import lax
from jax.experimental import pallas as pl
from jax.experimental.pallas import tpu as pltpu
from jax.sharding import PartitionSpec as P

MESH = pl.DeviceIdType.MESH
SIDE = 4
CHIPS = SIDE**3
DEVICES = 2 * CHIPS
GROUP = 8
EDGE_GROUP = 1

DISTANCES = sorted(itertools.product(range(SIDE // 2 + 1), repeat=3), key=lambda d: -sum(d))


def partners_at(distance, turn, me, visit):
    both_ways = [axis for axis, step in enumerate(distance) if step == 1]

    def one(number, carry):
        signs = dict.fromkeys(range(3), 1)
        for bit, axis in enumerate(both_ways):
            signs[axis] = 1 - 2 * ((number // 2**bit) % 2)
        steps = (turn, *(distance[axis] * signs[axis] + SIDE for axis in range(3)))
        core, y, x, z = ((at + step) % size for at, step, size in zip(me, steps, (2, SIDE, SIDE, SIDE)))
        visit((core, (y * SIDE + x) * SIDE + z))
        return carry

    if turn or any(distance):
        lax.fori_loop(0, 2 ** len(both_ways), one, 0)


def number_of(device):
    return device[0] * CHIPS + device[1]


def device_of(number):
    return number // CHIPS, number % CHIPS


def kernel(
    accum_hbm,
    slot_hbm,
    length_hbm,
    wet_hbm,
    count_hbm,
    out_ref,
    accum,
    slot,
    length_ref,
    send_0,
    send_1,
    send_2,
    recv_0,
    recv_1,
    recv_2,
    edge_rows,
    wet_send,
    wet_recv,
    picks,
    picks_smem,
    slot_smem,
    wet_smem,
    count_smem,
    from_smem,
    take_smem,
    keep_smem,
    load_sem,
    picks_sem,
    send_sem,
    recv_sem,
    wet_send_sem,
    wet_recv_sem,
):
    sends, recvs = (send_0, send_1, send_2), (recv_0, recv_1, recv_2)
    groups = len(sends)
    blocks, fields, cells = accum.shape
    core, chip = lax.axis_index("grp"), lax.axis_index("dev")
    me = (core, chip // (SIDE * SIDE), (chip // SIDE) % SIDE, chip % SIDE)
    mine = core * CHIPS + chip

    loads = [
        pltpu.make_async_copy(src, dst, load_sem.at[number])
        for number, (src, dst) in enumerate(
            (
                (slot_hbm, slot),
                (length_hbm, length_ref),
                (accum_hbm, accum),
                (count_hbm, count_smem),
                (wet_hbm, wet_smem),
                (slot_hbm, slot_smem),
            )
        )
    ]
    for load in loads:
        load.start()
    barrier = pltpu.get_barrier_semaphore()

    def greet(step, carry):
        other = device_of((mine + step) % DEVICES)
        pl.semaphore_signal(barrier, 1, device_id=other, device_id_type=MESH)
        return carry

    lax.fori_loop(1, DEVICES, greet, 0)

    for load in loads[:2]:
        load.wait()
    row = lax.broadcasted_iota(jnp.int32, (128, 128), 0)
    lane = lax.broadcasted_iota(jnp.int32, (128, 128), 1)
    length = length_ref[...]
    length_col = jnp.sum(jnp.where(row == lane, length, 0), axis=1, keepdims=True)
    end = jnp.sum(jnp.where(row <= lane, length_col, 0), axis=0, keepdims=True)
    start = end - length
    slots = slot[...]
    held = (slots >> 7) == mine
    column = jnp.sum(jnp.where(held, lane, 0), axis=1, keepdims=True)
    local = jnp.sum(jnp.where(held, slots & 127, 0), axis=1, keepdims=True)
    order = row * 128 + column - start
    inside = (order >= 0) & (order < length)
    ahead, behind = order == -1, order == length
    for number, chosen in enumerate((inside & (order < 128), inside & (order >= 128), ahead, behind)):
        picks[number : number + 1, :] = jnp.sum(jnp.where(chosen, local, 0), axis=0, keepdims=True)
    picks_copy = pltpu.make_async_copy(picks, picks_smem, picks_sem)
    picks_copy.start()
    has_ahead = jnp.sum(jnp.where(ahead, 1.0, 0.0), axis=0, keepdims=True)
    has_behind = jnp.sum(jnp.where(behind, 1.0, 0.0), axis=0, keepdims=True)
    at_me = lax.broadcasted_iota(jnp.int32, (1, 128), 1) == mine
    my_start = jnp.sum(jnp.where(at_me, start, 0))
    my_length = jnp.sum(jnp.where(at_me, length, 0))
    final = jnp.maximum(my_length, 1) - 1

    for load in loads[3:5]:
        load.wait()
    at_field = lax.broadcasted_iota(jnp.int32, (GROUP, cells), 0)
    scales = []
    for group in range(groups):
        count = jnp.ones((GROUP, cells), jnp.int32)
        for field in range(GROUP):
            count = jnp.where(at_field == field, count_smem[group * GROUP + field], count)
        scales.append(0.25 / count.astype(jnp.float32))

    def is_wet(index):
        return wet_smem[index >> 7, index & 127] == 1

    wet_send[0] = jnp.full((GROUP, cells), jnp.where(is_wet(final), 1.0, 0.0), jnp.float32)
    wet_send[1] = jnp.full((GROUP, cells), jnp.where(is_wet(0), 1.0, 0.0), jnp.float32)

    picks_copy.wait()
    loads[2].wait()

    def pack(group):
        fields_of = slice(group * GROUP, (group + 1) * GROUP)

        def one(owner, carry):
            for rank in range(2):
                block = accum[picks_smem[rank, owner], fields_of]
                sends[group][owner, rank * GROUP : (rank + 1) * GROUP] = block * scales[group]
            return carry

        lax.fori_loop(0, DEVICES, one, 0, unroll=16)

    def keep_mine(group):
        recvs[group][mine] = sends[group][mine]

    def post(stage):
        group, turn = divmod(stage, 2)

        def to(other):
            pltpu.make_async_remote_copy(
                src_ref=sends[group].at[number_of(other)],
                dst_ref=recvs[group].at[mine],
                send_sem=send_sem.at[stage],
                recv_sem=recv_sem.at[group],
                device_id=other,
                device_id_type=MESH,
            ).start()

        for distance in DISTANCES:
            partners_at(distance, turn, me, to)

    def sent(stage):
        group, turn = divmod(stage, 2)
        those = sends[group].at[pl.ds(0, CHIPS - 1 + turn)]
        pltpu.make_async_copy(those, those, send_sem.at[stage]).wait()

    pack(0)
    keep_mine(0)
    pl.semaphore_wait(barrier, DEVICES - 1)
    wet_copies = []
    for side, step in enumerate((1, DEVICES - 1)):
        copy = pltpu.make_async_remote_copy(
            src_ref=wet_send.at[side],
            dst_ref=wet_recv.at[side],
            send_sem=wet_send_sem.at[side],
            recv_sem=wet_recv_sem.at[side],
            device_id=device_of((mine + step) % DEVICES),
            device_id_type=MESH,
        )
        copy.start()
        wet_copies.append(copy)
    post(0)
    post(1)

    all_scales = jnp.concatenate(scales, axis=0)
    wide_lane = lax.broadcasted_iota(jnp.int32, (fields, cells), 1)

    def collect(owner, carry):
        cells_ahead, cells_behind = carry
        here = wide_lane == owner
        last = accum[picks_smem[2, owner]][:, cells - 1 : cells]
        first = accum[picks_smem[3, owner]][:, 0:1]
        return jnp.where(here, last, cells_ahead), jnp.where(here, first, cells_behind)

    nothing = jnp.zeros((fields, cells), jnp.float32)
    cells_ahead, cells_behind = lax.fori_loop(0, DEVICES, collect, (nothing, nothing), unroll=8)
    gathered = jnp.concatenate(
        [
            cells_ahead * all_scales * has_ahead,
            cells_behind * all_scales * has_behind,
            jnp.zeros((128 - 2 * fields, cells), jnp.float32),
        ],
        axis=0,
    )
    edge_rows[...] = gathered.T

    def attach(owner, carry):
        sends[EDGE_GROUP][owner, 2 * GROUP : 2 * GROUP + 1] = edge_rows[pl.ds(owner, 1)]
        return carry

    lax.fori_loop(0, DEVICES, attach, 0, unroll=16)
    for group in range(1, groups):
        pack(group)
        keep_mine(group)

    loads[5].wait()

    def table(index, carry):
        block = jnp.minimum(my_start + index, DEVICES * blocks - 1)
        behind_me = index == my_length
        from_smem[index] = jnp.where(behind_me, DEVICES, slot_smem[block >> 7, block & 127] >> 7)
        keep = jnp.where((index < my_length) & is_wet(index), 1.0, 0.0)
        keep_smem[index] = keep
        take_smem[index] = jnp.where(behind_me, 1.0, keep)
        return carry

    capacity = out_ref.shape[0]
    lax.fori_loop(0, capacity, table, 0, unroll=16)
    from_smem[capacity] = DEVICES
    take_smem[capacity] = 1.0

    at_lane = lax.broadcasted_iota(jnp.int32, (GROUP, cells), 1)
    first_lane, last_lane = at_lane == 0, at_lane == cells - 1

    def arrived(group):
        those = recvs[group].at[pl.ds(0, DEVICES - 1)]
        pltpu.make_async_copy(those, those, recv_sem.at[group]).wait()

    def edges():
        def add(sender, carry):
            return carry + recvs[EDGE_GROUP][sender, 2 * GROUP : 2 * GROUP + 1]

        total = lax.fori_loop(0, DEVICES, add, jnp.zeros((1, cells), jnp.float32), unroll=16)
        lefts = []
        for group in range(groups):
            left, right = (
                jnp.sum(jnp.where(at_lane == at_field + side * fields + group * GROUP, total, 0.0), axis=1, keepdims=True)
                for side in range(2)
            )
            lefts.append(left * wet_recv[0])
            for rank in range(2):
                recvs[group][DEVICES, rank * GROUP : (rank + 1) * GROUP] = right * wet_recv[1]
        return lefts

    def smooth(group, left):
        recv = recvs[group]
        fields_of = slice(group * GROUP, (group + 1) * GROUP)

        def value(index, rank):
            return recv[from_smem[index], rank * GROUP : (rank + 1) * GROUP] * take_smem[index]

        def both(block):
            return block, pltpu.roll(block, 1, 1), pltpu.roll(block, cells - 1, 1)

        def one(index, next_rank, carry):
            (current, to_right, to_left), previous = carry
            following = both(value(index + 1, next_rank))
            cell_before = jnp.where(first_lane, previous, to_right)
            cell_after = jnp.where(last_lane, following[2], to_left)
            out_ref[index, fields_of] = ((current + current) + (cell_before + cell_after)) * keep_smem[index]
            return following, to_right

        carry = (both(value(0, 0)), left)
        half = capacity // 2
        carry = lax.fori_loop(0, half - 1, lambda i, c: one(i, 0, c), carry, unroll=16)
        lax.fori_loop(half - 1, capacity, lambda i, c: one(i, 1, c), carry, unroll=16)

    for stage in range(2):
        sent(stage)
        post(stage + 2)
    arrived(0)
    for stage in range(2, 4):
        sent(stage)
        post(stage + 2)
    arrived(1)
    for copy in wet_copies:
        copy.wait()
    lefts = edges()
    smooth(0, lefts[0])
    smooth(1, lefts[1])
    arrived(2)
    smooth(2, lefts[2])
    sent(4)
    sent(5)


def on_device(accum, step_count, stretch_slot, span_length, wet_mask):
    blocks, fields, cells = accum.shape
    capacity = wet_mask.shape[0]
    groups = fields // GROUP
    heights = [2 * GROUP + (group == EDGE_GROUP) for group in range(groups)]
    arguments = (
        accum,
        stretch_slot.reshape(-1, 128),
        span_length.reshape(1, -1),
        wet_mask.reshape(-1, 128),
        step_count,
    )
    return pl.pallas_call(
        kernel,
        out_shape=pltpu.VMEM((capacity, fields, cells), jnp.float32),
        in_specs=[pl.BlockSpec(memory_space=pltpu.HBM)] * len(arguments),
        out_specs=pl.BlockSpec(memory_space=pltpu.VMEM),
        scratch_shapes=[
            pltpu.VMEM((blocks, fields, cells), jnp.float32),
            pltpu.VMEM((128, 128), jnp.int32),
            pltpu.VMEM((1, 128), jnp.int32),
            *[pltpu.VMEM((DEVICES, height, cells), jnp.float32) for height in heights],
            *[pltpu.VMEM((DEVICES + 1, height, cells), jnp.float32) for height in heights],
            pltpu.VMEM((128, cells), jnp.float32),
            pltpu.VMEM((2, GROUP, cells), jnp.float32),
            pltpu.VMEM((2, GROUP, cells), jnp.float32),
            pltpu.VMEM((4, 128), jnp.int32),
            pltpu.SMEM((4, 128), jnp.int32),
            pltpu.SMEM((128, 128), jnp.int32),
            pltpu.SMEM((capacity // 128, 128), jnp.int32),
            pltpu.SMEM((fields,), jnp.int32),
            pltpu.SMEM((capacity + 1,), jnp.int32),
            pltpu.SMEM((capacity + 1,), jnp.float32),
            pltpu.SMEM((capacity,), jnp.float32),
            pltpu.SemaphoreType.DMA((6,)),
            pltpu.SemaphoreType.DMA,
            pltpu.SemaphoreType.DMA((2 * groups,)),
            pltpu.SemaphoreType.DMA((groups,)),
            pltpu.SemaphoreType.DMA((2,)),
            pltpu.SemaphoreType.DMA((2,)),
        ],
        compiler_params=pltpu.CompilerParams(
            collective_id=0, has_side_effects=True, vmem_limit_bytes=32 * 1024 * 1024
        ),
        name="remap",
    )(*(pltpu.with_memory_space_constraint(a, pltpu.HBM) for a in arguments))


def solution(mesh):
    return jax.shard_map(
        on_device,
        mesh=mesh,
        in_specs=(P(("grp", "dev"), None, None), P(), P(), P(), P(("grp", "dev"))),
        out_specs=P(("grp", "dev"), None, None),
        check_vma=False,
    )
```

time: 127 us -> 56.5 us (0.44)
  the two profiles are of different devices: /device:TPU:1 before, /device:TPU:65 now
where the time goes in v2:
time: 56.5 us; the launch traced here: 56.4 us
  Pallas kernels  54.7 us (97%)
  local copies, waits for them, and re-layouts  1.67 us (3%)
    pallas_call x1, Pallas kernels, on_device(): pl.pallas_call(kernel, out_shape=pltpu.VMEM((capacity, fields, cells), jn...  54.7 us
    unnamed x1, local copies, waits for them, and re-layouts  1.67 us

profile of v2, /device:TPU:65, one launch (start us, length us, event | category | flops | bytes accessed | tf_op | source)
XLA Modules:
  0.0 56.4 jit_solution(12282478800379425706)
XLA Ops:
  0.0 54.7 %remap.1 = f32[256,24,128]{2,1,0:T(8,128)S(1)} custom-call(f32[128,24,128]{2,1,0:T(8,128)} %accum_hbm.1, s32[128,128]{1,0:T(8,128)} %bitcast.3, s32[1,128]{1,0:T(1,128)} %bitcast.5, s32[2,128]{1,0:T(2,128)} %bitcast.4, s32[24]{0:T(128)} %count_hbm.1), custom_call_target="tpu_custom_call" | custom-call | tf_op jit(solution)/shard_map/remap/pallas_call | solution.py:331
  54.7 1.7 %copy.7 = f32[256,24,128]{2,1,0:T(8,128)} copy(f32[256,24,128]{2,1,0:T(8,128)S(1)} %remap.1) | data formatting | bytes 6291456

commit v3 on v2

--- a/solution.py
+++ b/solution.py
@@ -294,8 +294,8 @@
 
         carry = (both(value(0, 0)), left)
         half = capacity // 2
-        carry = lax.fori_loop(0, half - 1, lambda i, c: one(i, 0, c), carry, unroll=16)
-        lax.fori_loop(half - 1, capacity, lambda i, c: one(i, 1, c), carry, unroll=16)
+        for index in range(capacity):
+            carry = one(index, 0 if index < half - 1 else 1, carry)
 
     for stage in range(2):
         sent(stage)

time: 56.5 us -> 51.5 us (0.912)
  the two profiles are of different devices: /device:TPU:65 before, /device:TPU:1 now
where the time goes in v3:
time: 51.5 us; the launch traced here: 51.4 us
  Pallas kernels  49.7 us (97%)
  local copies, waits for them, and re-layouts  1.67 us (3%)
    pallas_call x1, Pallas kernels, on_device(): pl.pallas_call(kernel, out_shape=pltpu.VMEM((capacity, fields, cells), jn...  49.7 us
    unnamed x1, local copies, waits for them, and re-layouts  1.67 us

profile of v3, /device:TPU:1, one launch (start us, length us, event | category | flops | bytes accessed | tf_op | source)
XLA Modules:
  0.0 51.4 jit_solution(14722164489025492474)
XLA Ops:
  0.0 49.7 %remap.1 = f32[256,24,128]{2,1,0:T(8,128)S(1)} custom-call(f32[128,24,128]{2,1,0:T(8,128)} %accum_hbm.1, s32[128,128]{1,0:T(8,128)} %bitcast.3, s32[1,128]{1,0:T(1,128)} %bitcast.5, s32[2,128]{1,0:T(2,128)} %bitcast.4, s32[24]{0:T(128)} %count_hbm.1), custom_call_target="tpu_custom_call" | custom-call | tf_op jit(solution)/shard_map/remap/pallas_call | solution.py:331
  49.7 1.7 %copy.7 = f32[256,24,128]{2,1,0:T(8,128)} copy(f32[256,24,128]{2,1,0:T(8,128)S(1)} %remap.1) | data formatting | bytes 6291456

commit v4 on v3

--- a/solution.py
+++ b/solution.py
@@ -14,23 +14,45 @@
 GROUP = 8
 EDGE_GROUP = 1
 
-DISTANCES = sorted(itertools.product(range(SIDE // 2 + 1), repeat=3), key=lambda d: -sum(d))
-
-
-def partners_at(distance, turn, me, visit):
-    both_ways = [axis for axis, step in enumerate(distance) if step == 1]
-
-    def one(number, carry):
-        signs = dict.fromkeys(range(3), 1)
-        for bit, axis in enumerate(both_ways):
-            signs[axis] = 1 - 2 * ((number // 2**bit) % 2)
-        steps = (turn, *(distance[axis] * signs[axis] + SIDE for axis in range(3)))
-        core, y, x, z = ((at + step) % size for at, step, size in zip(me, steps, (2, SIDE, SIDE, SIDE)))
-        visit((core, (y * SIDE + x) * SIDE + z))
+STEPS = sorted(
+    itertools.product(range(SIDE), repeat=3),
+    key=lambda steps: (2 not in steps, -sum(min(step, SIDE - step) for step in steps)),
+)
+FAR = sum(2 in steps for steps in STEPS)
+PACKED = [
+    sum((STEPS[at + k][0] * 16 + STEPS[at + k][1] * 4 + STEPS[at + k][2]) << (6 * k) for k in range(4))
+    for at in range(0, CHIPS, 4)
+]
+STAGES = [(0, (FAR, CHIPS), (0, 1)), (0, (0, FAR), (0, 1))] + [
+    (group, (0, CHIPS), (turn,)) for group in (1, 2) for turn in range(2)
+]
+
+
+def how_many(stage):
+    _, (low, high), turns = stage
+    return sum(high - low - (turn == 0 and high == CHIPS) for turn in turns)
+
+
+def visit_all(stage, me, visit):
+    _, (low, high), turns = stage
+    core, y, x, z = me
+
+    def one(index, carry):
+        number = PACKED[0]
+        for k, packed in enumerate(PACKED[1:], 1):
+            number = jnp.where(index >> 2 == k, packed, number)
+        number = number >> (6 * (index & 3))
+        chip = (((y + (number >> 4)) & 3) * SIDE + ((x + (number >> 2)) & 3)) * SIDE + ((z + number) & 3)
+        for turn in turns:
+            visit(((core + turn) & 1, chip))
         return carry
 
-    if turn or any(distance):
-        lax.fori_loop(0, 2 ** len(both_ways), one, 0)
+    if len(turns) == 1:
+        lax.fori_loop(low, min(high, CHIPS - (turns[0] == 0)), one, 0)
+        return
+    lax.fori_loop(low, min(high, CHIPS - 1), one, 0)
+    if high == CHIPS:
+        visit(((core + 1) & 1, (y * SIDE + x) * SIDE + z))
 
 
 def number_of(device):
@@ -74,6 +96,7 @@
     recv_sem,
     wet_send_sem,
     wet_recv_sem,
+    ready_sem,
 ):
     sends, recvs = (send_0, send_1, send_2), (recv_0, recv_1, recv_2)
     groups = len(sends)
@@ -99,12 +122,10 @@
         load.start()
     barrier = pltpu.get_barrier_semaphore()
 
-    def greet(step, carry):
-        other = device_of((mine + step) % DEVICES)
+    def greet(other):
         pl.semaphore_signal(barrier, 1, device_id=other, device_id_type=MESH)
-        return carry
-
-    lax.fori_loop(1, DEVICES, greet, 0)
+
+    visit_all(STAGES[0], me, greet)
 
     for load in loads[:2]:
         load.wait()
@@ -166,7 +187,7 @@
         recvs[group][mine] = sends[group][mine]
 
     def post(stage):
-        group, turn = divmod(stage, 2)
+        group = STAGES[stage][0]
 
         def to(other):
             pltpu.make_async_remote_copy(
@@ -178,17 +199,21 @@
                 device_id_type=MESH,
             ).start()
 
-        for distance in DISTANCES:
-            partners_at(distance, turn, me, to)
+        visit_all(STAGES[stage], me, to)
 
     def sent(stage):
-        group, turn = divmod(stage, 2)
-        those = sends[group].at[pl.ds(0, CHIPS - 1 + turn)]
-        pltpu.make_async_copy(those, those, send_sem.at[stage]).wait()
+        part = sends[STAGES[stage][0]].at[pl.ds(0, how_many(STAGES[stage]))]
+        pltpu.make_async_copy(part, part, send_sem.at[stage]).wait()
 
     pack(0)
     keep_mine(0)
-    pl.semaphore_wait(barrier, DEVICES - 1)
+    pl.semaphore_wait(barrier, how_many(STAGES[0]))
+    corners = [steps for steps in itertools.product(range(2), repeat=3) if any(steps)]
+    for steps in corners:
+        y, x, z = ((at + step) % SIDE for at, step in zip(me[1:], steps))
+        pl.semaphore_signal(
+            ready_sem, 1, device_id=(core, (y * SIDE + x) * SIDE + z), device_id_type=MESH
+        )
     wet_copies = []
     for side, step in enumerate((1, DEVICES - 1)):
         copy = pltpu.make_async_remote_copy(
@@ -202,6 +227,7 @@
         copy.start()
         wet_copies.append(copy)
     post(0)
+    pl.semaphore_wait(ready_sem, len(corners))
     post(1)
 
     all_scales = jnp.concatenate(scales, axis=0)
@@ -356,6 +382,7 @@
             pltpu.SemaphoreType.DMA((groups,)),
             pltpu.SemaphoreType.DMA((2,)),
             pltpu.SemaphoreType.DMA((2,)),
+            pltpu.SemaphoreType.REGULAR,
         ],
         compiler_params=pltpu.CompilerParams(
             collective_id=0, has_side_effects=True, vmem_limit_bytes=32 * 1024 * 1024

time: 51.5 us -> 49.1 us (0.953)
  Pallas kernels: 49.7 us -> 47.3 us
    pallas_call x1, Pallas kernels: 49.7 us -> 47.3 us  [on_device(): pl.pallas_call(kernel, out_shape=pltpu.VMEM((capacity, fields, cells), jn...]
where the time goes in v4:
time: 49.1 us; the launch traced here: 49 us
  Pallas kernels  47.3 us (96%)
  local copies, waits for them, and re-layouts  1.67 us (3%)
    pallas_call x1, Pallas kernels, on_device(): pl.pallas_call(kernel, out_shape=pltpu.VMEM((capacity, fields, cells), jn...  47.3 us
    unnamed x1, local copies, waits for them, and re-layouts  1.67 us

profile of v4, /device:TPU:1, one launch (start us, length us, event | category | flops | bytes accessed | tf_op | source)
XLA Modules:
  0.0 49.0 jit_solution(8102180101940341414)
XLA Ops:
  0.0 47.3 %remap.1 = f32[256,24,128]{2,1,0:T(8,128)S(1)} custom-call(f32[128,24,128]{2,1,0:T(8,128)} %accum_hbm.1, s32[128,128]{1,0:T(8,128)} %bitcast.3, s32[1,128]{1,0:T(1,128)} %bitcast.5, s32[2,128]{1,0:T(2,128)} %bitcast.4, s32[24]{0:T(128)} %count_hbm.1), custom_call_target="tpu_custom_call" | custom-call | tf_op jit(solution)/shard_map/remap/pallas_call | solution.py:357
  47.3 1.7 %copy.7 = f32[256,24,128]{2,1,0:T(8,128)} copy(f32[256,24,128]{2,1,0:T(8,128)S(1)} %remap.1) | data formatting | bytes 6291456

commit v5 on v4

--- a/solution.py
+++ b/solution.py
@@ -1,3 +1,4 @@
+import functools
 import itertools
 
 import jax
@@ -63,6 +64,58 @@
     return number // CHIPS, number % CHIPS
 
 
+def smooth(recv, out, first_field, left, tables, slots, carry=None):
+    from_smem, take_smem, keep_smem = tables
+    capacity, cells = out.shape[0], out.shape[2]
+    at_lane = lax.broadcasted_iota(jnp.int32, (GROUP, cells), 1)
+    first_lane, last_lane = at_lane == 0, at_lane == cells - 1
+
+    def both(index):
+        rank = int(index >= capacity // 2)
+        block = recv[from_smem[index], rank * GROUP : (rank + 1) * GROUP] * take_smem[index]
+        return block, pltpu.roll(block, 1, 1), pltpu.roll(block, cells - 1, 1)
+
+    if carry is None:
+        carry = both(0), left
+    for index in slots:
+        (current, to_right, to_left), previous = carry
+        following = both(index + 1)
+        cell_before = jnp.where(first_lane, previous, to_right)
+        cell_after = jnp.where(last_lane, following[2], to_left)
+        smoothed = ((current + current) + (cell_before + cell_after)) * keep_smem[index]
+        out[index, first_field : first_field + GROUP] = smoothed
+        carry = following, to_right
+    return carry
+
+
+def finish(parts, done, recv, left, from_smem, take_smem, keep_smem, out_hbm, last, done_sem, last_sem):
+    capacity, ready, _ = done.shape
+    rows = capacity // parts
+    whole = [
+        pltpu.make_async_copy(
+            done.at[pl.ds(part * rows, rows)],
+            out_hbm.at[pl.ds(part * rows, rows), pl.ds(0, ready)],
+            done_sem.at[part],
+        )
+        for part in range(parts)
+    ]
+    for copy in whole:
+        copy.start()
+    carry, rest = None, []
+    for part in range(parts):
+        slots = range(part * rows, (part + 1) * rows)
+        carry = smooth(recv, last, 0, left[...], (from_smem, take_smem, keep_smem), slots, carry)
+        copy = pltpu.make_async_copy(
+            last.at[pl.ds(part * rows, rows)],
+            out_hbm.at[pl.ds(part * rows, rows), pl.ds(ready, GROUP)],
+            last_sem.at[part],
+        )
+        copy.start()
+        rest.append(copy)
+    for copy in whole + rest:
+        copy.wait()
+
+
 def kernel(
     accum_hbm,
     slot_hbm,
@@ -70,6 +123,11 @@
     wet_hbm,
     count_hbm,
     out_ref,
+    recv_2,
+    left_ref,
+    from_smem,
+    take_smem,
+    keep_smem,
     accum,
     slot,
     length_ref,
@@ -78,7 +136,6 @@
     send_2,
     recv_0,
     recv_1,
-    recv_2,
     edge_rows,
     wet_send,
     wet_recv,
@@ -87,9 +144,6 @@
     slot_smem,
     wet_smem,
     count_smem,
-    from_smem,
-    take_smem,
-    keep_smem,
     load_sem,
     picks_sem,
     send_sem,
@@ -300,29 +354,6 @@
                 recvs[group][DEVICES, rank * GROUP : (rank + 1) * GROUP] = right * wet_recv[1]
         return lefts
 
-    def smooth(group, left):
-        recv = recvs[group]
-        fields_of = slice(group * GROUP, (group + 1) * GROUP)
-
-        def value(index, rank):
-            return recv[from_smem[index], rank * GROUP : (rank + 1) * GROUP] * take_smem[index]
-
-        def both(block):
-            return block, pltpu.roll(block, 1, 1), pltpu.roll(block, cells - 1, 1)
-
-        def one(index, next_rank, carry):
-            (current, to_right, to_left), previous = carry
-            following = both(value(index + 1, next_rank))
-            cell_before = jnp.where(first_lane, previous, to_right)
-            cell_after = jnp.where(last_lane, following[2], to_left)
-            out_ref[index, fields_of] = ((current + current) + (cell_before + cell_after)) * keep_smem[index]
-            return following, to_right
-
-        carry = (both(value(0, 0)), left)
-        half = capacity // 2
-        for index in range(capacity):
-            carry = one(index, 0 if index < half - 1 else 1, carry)
-
     for stage in range(2):
         sent(stage)
         post(stage + 2)
@@ -334,10 +365,11 @@
     for copy in wet_copies:
         copy.wait()
     lefts = edges()
-    smooth(0, lefts[0])
-    smooth(1, lefts[1])
+    for group in range(2):
+        tables = from_smem, take_smem, keep_smem
+        smooth(recvs[group], out_ref, group * GROUP, lefts[group], tables, range(capacity))
+    left_ref[...] = jnp.broadcast_to(lefts[2], left_ref.shape)
     arrived(2)
-    smooth(2, lefts[2])
     sent(4)
     sent(5)
 
@@ -354,17 +386,24 @@
         wet_mask.reshape(-1, 128),
         step_count,
     )
-    return pl.pallas_call(
+    outcome = pl.pallas_call(
         kernel,
-        out_shape=pltpu.VMEM((capacity, fields, cells), jnp.float32),
+        out_shape=(
+            pltpu.VMEM((capacity, fields - GROUP, cells), jnp.float32),
+            pltpu.VMEM((DEVICES + 1, heights[2], cells), jnp.float32),
+            pltpu.VMEM((GROUP, cells), jnp.float32),
+            pltpu.SMEM((capacity + 1,), jnp.int32),
+            pltpu.SMEM((capacity + 1,), jnp.float32),
+            pltpu.SMEM((capacity,), jnp.float32),
+        ),
         in_specs=[pl.BlockSpec(memory_space=pltpu.HBM)] * len(arguments),
-        out_specs=pl.BlockSpec(memory_space=pltpu.VMEM),
+        out_specs=[pl.BlockSpec(memory_space=pltpu.VMEM)] * 3 + [pl.BlockSpec(memory_space=pltpu.SMEM)] * 3,
         scratch_shapes=[
             pltpu.VMEM((blocks, fields, cells), jnp.float32),
             pltpu.VMEM((128, 128), jnp.int32),
             pltpu.VMEM((1, 128), jnp.int32),
             *[pltpu.VMEM((DEVICES, height, cells), jnp.float32) for height in heights],
-            *[pltpu.VMEM((DEVICES + 1, height, cells), jnp.float32) for height in heights],
+            *[pltpu.VMEM((DEVICES + 1, height, cells), jnp.float32) for height in heights[:2]],
             pltpu.VMEM((128, cells), jnp.float32),
             pltpu.VMEM((2, GROUP, cells), jnp.float32),
             pltpu.VMEM((2, GROUP, cells), jnp.float32),
@@ -373,9 +412,6 @@
             pltpu.SMEM((128, 128), jnp.int32),
             pltpu.SMEM((capacity // 128, 128), jnp.int32),
             pltpu.SMEM((fields,), jnp.int32),
-            pltpu.SMEM((capacity + 1,), jnp.int32),
-            pltpu.SMEM((capacity + 1,), jnp.float32),
-            pltpu.SMEM((capacity,), jnp.float32),
             pltpu.SemaphoreType.DMA((6,)),
             pltpu.SemaphoreType.DMA,
             pltpu.SemaphoreType.DMA((2 * groups,)),
@@ -390,6 +426,24 @@
         name="remap",
     )(*(pltpu.with_memory_space_constraint(a, pltpu.HBM) for a in arguments))
 
+    parts = 4
+    return pl.pallas_call(
+        functools.partial(finish, parts),
+        out_shape=pltpu.HBM((capacity, fields, cells), jnp.float32),
+        in_specs=[pl.BlockSpec(memory_space=pltpu.VMEM)] * 3 + [pl.BlockSpec(memory_space=pltpu.SMEM)] * 3,
+        out_specs=pl.BlockSpec(memory_space=pltpu.HBM),
+        scratch_shapes=[
+            pltpu.VMEM((capacity, GROUP, cells), jnp.float32),
+            pltpu.SemaphoreType.DMA((parts,)),
+            pltpu.SemaphoreType.DMA((parts,)),
+        ],
+        compiler_params=pltpu.CompilerParams(vmem_limit_bytes=16 * 1024 * 1024),
+        name="finish",
+    )(
+        *(pltpu.with_memory_space_constraint(a, pltpu.VMEM) for a in outcome[:3]),
+        *(pltpu.with_memory_space_constraint(a, pltpu.SMEM) for a in outcome[3:]),
+    )
+
 
 def solution(mesh):
     return jax.shard_map(

time: 49.1 us -> 48.7 us (level)
  local copies, waits for them, and re-layouts: 1.67 us -> 0 us
  Pallas kernels: 47.3 us -> 48.6 us
    unnamed x1 -> x0, local copies, waits for them, and re-layouts: 1.67 us -> none
    pallas_call x1 -> x2, Pallas kernels: 47.3 us -> 48.6 us  [the longest x1 46.7 us: on_device(): pl.pallas_call(kernel, out_shape=(pltpu.VMEM((capacity, fields - GROUP, c...]
where the time goes in v5:
time: 48.7 us; the launch traced here: 48.6 us
  Pallas kernels  48.6 us (100%)
    pallas_call x1, Pallas kernels, on_device(): pl.pallas_call(kernel, out_shape=(pltpu.VMEM((capacity, fields - GROUP, c...  46.7 us
    pallas_call x1, Pallas kernels, on_device(): pl.pallas_call(functools.partial(finish, parts), out_shape=pltpu.HBM((cap...  1.88 us

profile of v5, /device:TPU:1, one launch (start us, length us, event | category | flops | bytes accessed | tf_op | source)
XLA Modules:
  0.0 48.6 jit_solution(3832177496141516658)
XLA Ops:
  0.0 46.7 %remap.1 = (f32[256,16,128]{2,1,0:T(8,128)S(1)}, f32[129,16,128]{2,1,0:T(8,128)S(1)}, f32[8,128]{1,0:T(8,128)S(1)}, s32[257]{0:T(512)S(4)}, f32[257]{0:T(512)S(4)}, /*index=5*/f32[256]{0:T(256)S(4)}) custom-call(f32[128,24,128]{2,1,0:T(8,128)} %accum_hbm.1, s32[128,128]{1,0:T(8,128)} %bitcast.3, s32[1,128]{1,0:T(1,128)} %bitcast.5, s32[2,128]{1,0:T(2,128)} %bitcast.4, ...), custom_call_target="tpu_custom_call" | custom-call | tf_op jit(solution)/shard_map/remap/pallas_call | solution.py:389
  46.7 1.9 %finish.1 = f32[256,24,128]{2,1,0:T(8,128)} custom-call(f32[256,16,128]{2,1,0:T(8,128)S(1)} %get-tuple-element.11.done, f32[129,16,128]{2,1,0:T(8,128)S(1)} %get-tuple-element.12.recv, f32[8,128]{1,0:T(8,128)S(1)} %get-tuple-element.13.left, s32[257]{0:T(512)S(4)} %get-tuple-element.14.from_smem, f32[257]{0:T(512)S(4)} %get-tuple-element.15.take_smem, ...), custom_call_target="tpu_custom_call" | custom-call | tf_op jit(solution)/shard_map/finish/pallas_call | solution.py:430

commit v6 on v5

--- a/solution.py
+++ b/solution.py
@@ -426,7 +426,7 @@
         name="remap",
     )(*(pltpu.with_memory_space_constraint(a, pltpu.HBM) for a in arguments))
 
-    parts = 4
+    parts = 8
     return pl.pallas_call(
         functools.partial(finish, parts),
         out_shape=pltpu.HBM((capacity, fields, cells), jnp.float32),

time: 48.7 us -> 48.7 us (level)
  no operation moved by 1% of the time
where the time goes in v6:
time: 48.7 us; the launch traced here: 48.6 us
  Pallas kernels  48.6 us (100%)
    pallas_call x1, Pallas kernels, on_device(): pl.pallas_call(kernel, out_shape=(pltpu.VMEM((capacity, fields - GROUP, c...  46.7 us
    pallas_call x1, Pallas kernels, on_device(): pl.pallas_call(functools.partial(finish, parts), out_shape=pltpu.HBM((cap...  1.89 us

profile of v6, /device:TPU:1, one launch (start us, length us, event | category | flops | bytes accessed | tf_op | source)
XLA Modules:
  0.0 48.6 jit_solution(9942126718678151487)
XLA Ops:
  0.0 46.7 %remap.1 = (f32[256,16,128]{2,1,0:T(8,128)S(1)}, f32[129,16,128]{2,1,0:T(8,128)S(1)}, f32[8,128]{1,0:T(8,128)S(1)}, s32[257]{0:T(512)S(4)}, f32[257]{0:T(512)S(4)}, /*index=5*/f32[256]{0:T(256)S(4)}) custom-call(f32[128,24,128]{2,1,0:T(8,128)} %accum_hbm.1, s32[128,128]{1,0:T(8,128)} %bitcast.3, s32[1,128]{1,0:T(1,128)} %bitcast.5, s32[2,128]{1,0:T(2,128)} %bitcast.4, ...), custom_call_target="tpu_custom_call" | custom-call | tf_op jit(solution)/shard_map/remap/pallas_call | solution.py:389
  46.7 1.9 %finish.1 = f32[256,24,128]{2,1,0:T(8,128)} custom-call(f32[256,16,128]{2,1,0:T(8,128)S(1)} %get-tuple-element.11.done, f32[129,16,128]{2,1,0:T(8,128)S(1)} %get-tuple-element.12.recv, f32[8,128]{1,0:T(8,128)S(1)} %get-tuple-element.13.left, s32[257]{0:T(512)S(4)} %get-tuple-element.14.from_smem, f32[257]{0:T(512)S(4)} %get-tuple-element.15.take_smem, ...), custom_call_target="tpu_custom_call" | custom-call | tf_op jit(solution)/shard_map/finish/pallas_call | solution.py:430

commit v7 on v6

--- a/solution.py
+++ b/solution.py
@@ -426,7 +426,7 @@
         name="remap",
     )(*(pltpu.with_memory_space_constraint(a, pltpu.HBM) for a in arguments))
 
-    parts = 8
+    parts = 16
     return pl.pallas_call(
         functools.partial(finish, parts),
         out_shape=pltpu.HBM((capacity, fields, cells), jnp.float32),

time: 48.7 us -> 48.8 us (level)
  no operation moved by 1% of the time
where the time goes in v7:
time: 48.8 us; the launch traced here: 48.7 us
  Pallas kernels  48.7 us (100%)
    pallas_call x1, Pallas kernels, on_device(): pl.pallas_call(kernel, out_shape=(pltpu.VMEM((capacity, fields - GROUP, c...  46.7 us
    pallas_call x1, Pallas kernels, on_device(): pl.pallas_call(functools.partial(finish, parts), out_shape=pltpu.HBM((cap...  2.01 us

profile of v7, /device:TPU:1, one launch (start us, length us, event | category | flops | bytes accessed | tf_op | source)
XLA Modules:
  0.0 48.7 jit_solution(17255872926866120420)
XLA Ops:
  0.0 46.7 %remap.1 = (f32[256,16,128]{2,1,0:T(8,128)S(1)}, f32[129,16,128]{2,1,0:T(8,128)S(1)}, f32[8,128]{1,0:T(8,128)S(1)}, s32[257]{0:T(512)S(4)}, f32[257]{0:T(512)S(4)}, /*index=5*/f32[256]{0:T(256)S(4)}) custom-call(f32[128,24,128]{2,1,0:T(8,128)} %accum_hbm.1, s32[128,128]{1,0:T(8,128)} %bitcast.3, s32[1,128]{1,0:T(1,128)} %bitcast.5, s32[2,128]{1,0:T(2,128)} %bitcast.4, ...), custom_call_target="tpu_custom_call" | custom-call | tf_op jit(solution)/shard_map/remap/pallas_call | solution.py:389
  46.7 2.0 %finish.1 = f32[256,24,128]{2,1,0:T(8,128)} custom-call(f32[256,16,128]{2,1,0:T(8,128)S(1)} %get-tuple-element.11.done, f32[129,16,128]{2,1,0:T(8,128)S(1)} %get-tuple-element.12.recv, f32[8,128]{1,0:T(8,128)S(1)} %get-tuple-element.13.left, s32[257]{0:T(512)S(4)} %get-tuple-element.14.from_smem, f32[257]{0:T(512)S(4)} %get-tuple-element.15.take_smem, ...), custom_call_target="tpu_custom_call" | custom-call | tf_op jit(solution)/shard_map/finish/pallas_call | solution.py:430
